TPU v7x, 256 devices: a whole 4x4x8 slice. The times are simulated.
256 devices in a mesh: rep: 16 (over x, z_hi, core), stripe: 16 (over y, z_lo).
Axes of the slice: x: 4, y: 4, z: 8 (z_hi: 2, z_lo: 4; z = z_hi * 4 + z_lo), core: 2. Of those that a mesh axis runs over, the one named last changes fastest.
Arguments:
- activations: bfloat16 [4096, 4096], P('rep'), may hold values from -6 to 6
- out_grads: bfloat16 [4096, 8192], P('rep', 'stripe'), may hold values from -4 to 4
- statistics: float32 [16, 16, 512, 512], P('rep', 'stripe'), may hold values from -48 to 4608, as said below
- owner_blocks: int32 [16, 8], P('stripe'), may hold values from 0 to 7, each once within a row
Outputs:
- preconditioned: float32 [4096, 8192], P(None, 'stripe')
- new_stats: float32 [16, 16, 512, 512], P('rep', 'stripe')
Inputs may be any that keep to these rules, and one draw needn't show every extreme that they name: statistics[p, s] is symmetric positive definite for every p and s. `owner_blocks`: each row lists every row block 0 to 7 exactly once.
All inputs are finite; a program needn't handle non-finite values.
Results may differ from a plain program's by a relative error of at most 0.0003.
Values sent between devices are 32-bit elements; how exact they have to be, the bound alone decides.
A program may use at most 128 MiB of HBM per device.

v0:
```python
import jax
import jax.numpy as jnp
from jax import lax
from jax.sharding import Mesh
from jax.sharding import PartitionSpec as P

BLOCK = 512
ITERS = 2
REP = ("rep_0", "rep_1", "rep_2")
REP_STRIPE = ("rep_0", "rep_1", "rep_2", "stripe_0", "stripe_1")
STRIPE = ("stripe_0", "stripe_1")
decay_rate = 0.95
damping = 0.25
epsilon = 1e-06
highest = lax.Precision.HIGHEST


def partner(shard, axis, stride):
    return lax.ppermute(shard, axis, [(i, i ^ 1 << stride) for i in range(lax.axis_size(axis))])


def by_axis(shard, axes):
    for axis in axes:
        shard = lax.psum(shard, axis)
    return shard


def inverse_root(damped):
    identity = jnp.eye(damped.shape[-1], dtype=damped.dtype)
    frob_norm = jnp.sqrt(jnp.sum(damped * damped, axis=(-2, -1), keepdims=True) + epsilon)
    scaled = damped / frob_norm
    root_now = identity * frob_norm ** (-0.25)
    for sweep in range(ITERS):
        factor = (5.0 * identity - scaled) * 0.25
        root_now = jnp.matmul(root_now, factor, precision=highest)
        if sweep + 1 < ITERS:
            square = jnp.matmul(factor, factor, precision=highest)
            fourth = jnp.matmul(square, square, precision=highest)
            scaled = jnp.matmul(fourth, scaled, precision=highest)
    return root_now


def slot_terms(activations, out_grads, blocks_of, pair_count, piece_rows, row_count):
    tokens_here, in_width = activations.shape
    per_block = BLOCK // piece_rows
    shaped = activations.reshape(tokens_here, in_width // piece_rows, piece_rows)
    slot_count = row_count // piece_rows
    slot_ids = jnp.arange(slot_count, dtype=jnp.int32)
    block_ids = jnp.take(blocks_of, slot_ids % pair_count)
    half_ids = slot_ids // pair_count % per_block
    chosen = jnp.take(shaped, block_ids * per_block + half_ids, axis=1)
    products = jnp.einsum("tkp,tc->kpc", chosen, out_grads, preferred_element_type=jnp.float32)
    return products.reshape(slot_count * piece_rows, out_grads.shape[1])


def per_device(activations, out_grads, statistics, owner_blocks):
    rep_count = lax.axis_size(REP)
    pair_count = rep_count // 2
    pair_bit = rep_count.bit_length() - 2
    half_rows = BLOCK // 2
    my_index = lax.axis_index(REP)
    is_left = my_index < pair_count
    blocks_of = owner_blocks[0]
    own_half = lax.psum_scatter(
        slot_terms(
            activations, out_grads, blocks_of, pair_count, half_rows, half_rows * lax.axis_size(REP)
        ),
        REP,
        scatter_dimension=0,
        tiled=True,
    )
    partner_half = partner(own_half, REP, pair_bit)
    gradient = jnp.where(
        is_left,
        jnp.concatenate([own_half, partner_half], axis=0),
        jnp.concatenate([partner_half, own_half], axis=0),
    )
    facing = jnp.where(is_left, gradient, gradient.T)
    new_stat = decay_rate * statistics[0, 0] + jnp.dot(facing, facing.T, precision=highest)
    trace_sum = by_axis(jnp.trace(new_stat), REP_STRIPE)
    mean_diag = trace_sum / (rep_count * lax.axis_size(STRIPE) * BLOCK)
    identity = jnp.eye(BLOCK, dtype=jnp.float32)
    root_now = inverse_root(new_stat + damping * mean_diag * identity)
    partner_root = partner(root_now, REP, pair_bit)
    left_root = jnp.where(is_left, root_now, partner_root)
    right_root = jnp.where(is_left, partner_root, root_now)
    row_start = jnp.where(is_left, 0, half_rows).astype(jnp.int32)
    my_rows = lax.dynamic_slice_in_dim(left_root, row_start, half_rows, 0)
    grad_rows = lax.dynamic_slice_in_dim(gradient, row_start, half_rows, 0)
    precond_half = jnp.dot(
        jnp.dot(my_rows, gradient, precision=highest), right_root, precision=highest
    )
    grad_sq, prec_sq = (
        by_axis(jnp.sum(grad_rows * grad_rows), REP_STRIPE),
        by_axis(jnp.sum(precond_half * precond_half), REP_STRIPE),
    )
    scaled = precond_half * jnp.sqrt(grad_sq / (prec_sq + epsilon))
    gathered = lax.all_gather(scaled[None], REP, axis=0, tiled=True)
    pair_ids = jnp.arange(pair_count, dtype=jnp.int32)
    inverse = jnp.sum(
        pair_ids[:, None] * (blocks_of[:, None] == pair_ids[None, :]).astype(jnp.int32), axis=0
    )
    row_order = jnp.stack([inverse, inverse + pair_count], axis=1).reshape(-1)
    preconditioned = jnp.take(gathered, row_order, axis=0).reshape(
        pair_count * BLOCK, gathered.shape[2]
    )
    return (preconditioned, new_stat[None, None])


def solution(mesh):
    split = Mesh(
        mesh.devices.reshape(4, 2, 2, 4, 4), ("rep_0", "rep_1", "rep_2", "stripe_0", "stripe_1")
    )
    return jax.shard_map(
        per_device,
        mesh=split,
        in_specs=(P(REP, None), P(REP, STRIPE), P(REP, STRIPE, None, None), P(STRIPE, None)),
        out_specs=(P(None, STRIPE), P(REP, STRIPE, None, None)),
        check_vma=False,
    )
```

profile of v0, /device:TPU:1, one launch (start us, length us, event | category | flops | bytes accessed | tf_op | source)
XLA Modules:
  0.0 449.1 jit_solution(16025409931431591571)
XLA Ops:
  7.2 0.0 copy-start
  7.2 0.0 reduce-scatter.2.cloned.1.call-start
  7.2 0.8 select_reduce_fusion.1
  8.0 0.1 copy.25
  8.1 0.1 reshape.203
  8.2 1.3 gather_fusion
  9.6 4.1 copy.26
  13.7 2.8 copy.27
  16.5 2.0 gather_fusion.1
  18.5 6.7 %fusion = f32[16,256,512]{2,1,0:T(8,128)} fusion(bf16[16,256,256]{2,1,0:T(8,128)(2,1)} %gather_fusion.1, pred[16]{0:T(512)(128)(4,1)S(1)} %get-tuple-element.16, bf16[256,512]{1,0:T(8,128)(2,1)S(1)} %copy-done), kind=kOutput, calls=%fused_computation.4 | convolution fusion | flops 1074790400 | bytes 10747920 | tf_op jit(solution)/shard_map/tkp,tc->kpc/dot_general | solution.py:52
  25.2 8.9 %copy.29 = f32[4096,512]{0,1:T(8,128)} copy(f32[4096,512]{1,0:T(8,128)} %bitcast.40) | data formatting | bytes 16777216 | tf_op jit(solution)/shard_map/reshape | solution.py:53
  34.1 0.0 reduce-scatter.2.cloned.1.call-update
  34.2 0.0 all-gather.3.cloned.1.call-start
  34.2 142.1 %reduce-scatter.2.cloned.1.call-done = f32[256,512]{0,1:T(8,128)} async-done(((f32[4096,512]{0,1:T(8,128)}), f32[256,512]{0,1:T(8,128)}) %reduce-scatter.2.cloned.1.call-update) | async-done | bytes 524304 | tf_op jit(solution)/shard_map/reduce_scatter | solution.py:64
  176.3 1.2 collective-permute-start
  177.5 11.7 %collective-permute-done = f32[256,512]{0,1:T(8,128)S(1)} collective-permute-done((f32[256,512]{0,1:T(8,128)}, f32[256,512]{0,1:T(8,128)S(1)}, u32[]{:S(2)}, u32[]{:S(2)}) %collective-permute-start) | collective-permute-done | bytes 524320 | tf_op jit(solution)/shard_map/ppermute | solution.py:19
  189.3 1.6 maximum_select_fusion
  190.9 0.3 copy.31
  191.2 5.6 %select_reduce_fusion = (f32[]{:T(128)}, f32[512,512]{1,0:T(8,128)S(1)}) fusion(f32[512,512]{1,0:T(8,128)S(1)} %copy.31, pred[]{:T(512)S(6)} %lt.75, f32[256,512]{0,1:T(8,128)} %reduce-scatter.2.cloned.1.call-done, f32[256,512]{0,1:T(8,128)} %copy-done.3, f32[1,1,512,512]{3,2,1,0:T(8,128)} %param.6), kind=kOutput, calls=%fused_computation.22 | convolution fusion | flops 1612972032 | bytes 4194309 | tf_op jit(solution)/shard_map/dot_general | solution.py:79
  196.8 6.6 %psum.105 = f32[]{:T(128)} all-reduce(f32[]{:T(128)} %get-tuple-element.12), channel_id=1, replica_groups=mesh['rep_0'=4,'rep_1'=2,'rep_2'=2,'stripe_0'=4,'stripe_1'=4] {'rep_0'}, use_global_device_ids=true, to_apply=%region_3.4 | all-reduce | flops 1 | bytes 8 | tf_op jit(solution)/shard_map/psum | solution.py:24
  203.4 8.3 %psum.106 = f32[]{:T(128)} all-reduce(f32[]{:T(128)} %psum.105), channel_id=1, replica_groups=mesh['rep_0'=4,'rep_1'=2,'rep_2'=2,'stripe_0'=4,'stripe_1'=4] {'rep_1'}, use_global_device_ids=true, to_apply=%region_4.5 | all-reduce | flops 1 | bytes 8 | tf_op jit(solution)/shard_map/psum | solution.py:24
  211.6 9.8 %psum.107 = f32[]{:T(128)} all-reduce(f32[]{:T(128)} %psum.106), channel_id=1, replica_groups=mesh['rep_0'=4,'rep_1'=2,'rep_2'=2,'stripe_0'=4,'stripe_1'=4] {'rep_2'}, use_global_device_ids=true, to_apply=%region_5.6 | all-reduce | flops 1 | bytes 8 | tf_op jit(solution)/shard_map/psum | solution.py:24
  221.4 7.5 %psum.108 = f32[]{:T(128)} all-reduce(f32[]{:T(128)} %psum.107), channel_id=1, replica_groups=mesh['rep_0'=4,'rep_1'=2,'rep_2'=2,'stripe_0'=4,'stripe_1'=4] {'stripe_0'}, use_global_device_ids=true, to_apply=%region_6.7 | all-reduce | flops 1 | bytes 8 | tf_op jit(solution)/shard_map/psum | solution.py:24
  228.9 10.8 %psum.109 = f32[]{:T(128)} all-reduce(f32[]{:T(128)} %psum.108), channel_id=1, replica_groups=mesh['rep_0'=4,'rep_1'=2,'rep_2'=2,'stripe_0'=4,'stripe_1'=4] {'stripe_1'}, use_global_device_ids=true, to_apply=%region_7.8 | all-reduce | flops 1 | bytes 8 | tf_op jit(solution)/shard_map/psum | solution.py:24
  240.3 1.0 multiply_reduce_fusion
  242.0 2.0 fusion.12
  244.0 0.0 copy-start.2
  244.0 1.8 fusion.46
  245.8 1.9 fusion.4
  247.8 3.1 fusion.9
  250.9 1.8 fusion.47
  252.8 0.7 collective-permute-start.1
  253.4 0.7 multiply_reduce_fusion.2
  254.2 20.9 %collective-permute-done.1 = f32[512,512]{1,0:T(8,128)S(1)} collective-permute-done((f32[512,512]{1,0:T(8,128)S(1)}, f32[512,512]{1,0:T(8,128)S(1)}, u32[]{:S(2)}, u32[]{:S(2)}) %collective-permute-start.1) | collective-permute-done | bytes 1048608 | tf_op jit(solution)/shard_map/ppermute | solution.py:19
  275.0 2.7 fusion.15
  277.8 1.8 multiply_reduce_fusion.1
  279.5 6.6 %all-reduce.2 = (f32[]{:T(128)}, f32[]{:T(128)}) all-reduce(f32[]{:T(128)} %multiply_reduce_fusion.2, f32[]{:T(128)} %get-tuple-element.14), channel_id=1, replica_groups=mesh['rep_0'=4,'rep_1'=2,'rep_2'=2,'stripe_0'=4,'stripe_1'=4] {'rep_0'}, use_global_device_ids=true, to_apply=%region_10.11 | all-reduce | flops 2 | bytes 16 | tf_op jit(solution)/shard_map/psum | solution.py:24
  286.1 8.4 %all-reduce.4 = (f32[]{:T(128)}, f32[]{:T(128)}) all-reduce(f32[]{:T(128)} %get-tuple-element.6, f32[]{:T(128)} %get-tuple-element.7), channel_id=1, replica_groups=mesh['rep_0'=4,'rep_1'=2,'rep_2'=2,'stripe_0'=4,'stripe_1'=4] {'rep_1'}, use_global_device_ids=true, to_apply=%region_11.12 | all-reduce | flops 2 | bytes 16 | tf_op jit(solution)/shard_map/psum | solution.py:24
  294.5 10.6 %all-reduce.3 = (f32[]{:T(128)}, f32[]{:T(128)}) all-reduce(f32[]{:T(128)} %get-tuple-element.10, f32[]{:T(128)} %get-tuple-element.11), channel_id=1, replica_groups=mesh['rep_0'=4,'rep_1'=2,'rep_2'=2,'stripe_0'=4,'stripe_1'=4] {'rep_2'}, use_global_device_ids=true, to_apply=%region_12.13 | all-reduce | flops 2 | bytes 16 | tf_op jit(solution)/shard_map/psum | solution.py:24
  305.1 6.8 %all-reduce.1 = (f32[]{:T(128)}, f32[]{:T(128)}) all-reduce(f32[]{:T(128)} %get-tuple-element.8, f32[]{:T(128)} %get-tuple-element.9), channel_id=1, replica_groups=mesh['rep_0'=4,'rep_1'=2,'rep_2'=2,'stripe_0'=4,'stripe_1'=4] {'stripe_0'}, use_global_device_ids=true, to_apply=%region_13.14 | all-reduce | flops 2 | bytes 16 | tf_op jit(solution)/shard_map/psum | solution.py:24
  311.8 7.2 %all-reduce = (f32[]{:T(128)}, f32[]{:T(128)}) all-reduce(f32[]{:T(128)} %get-tuple-element.4, f32[]{:T(128)} %get-tuple-element.5), channel_id=1, replica_groups=mesh['rep_0'=4,'rep_1'=2,'rep_2'=2,'stripe_0'=4,'stripe_1'=4] {'stripe_1'}, use_global_device_ids=true, to_apply=%region_14.15 | all-reduce | flops 2 | bytes 16 | tf_op jit(solution)/shard_map/psum | solution.py:24
  320.3 0.8 broadcast_multiply_fusion
  321.2 0.0 all-gather.3.cloned.1.call-update
  321.2 0.1 reshape.206
  321.3 0.1 broadcast_in_dim.39
  321.4 107.2 %all-gather.3.cloned.1.call-done = f32[4096,512]{1,0:T(8,128)} async-done(((f32[256,512]{1,0:T(8,128)}), f32[4096,512]{1,0:T(8,128)}) %all-gather.3.cloned.1.call-update) | async-done | bytes 8388624 | tf_op jit(solution)/shard_map/all_gather | solution.py:98
  428.6 7.7 %gather_fusion.2 = f32[16,256,512]{2,1,0:T(8,128)} fusion(f32[16,256,512]{2,1,0:T(8,128)} %bitcast.41, s32[1024]{0:T(1024)S(1)} %pad_clamp_fusion), kind=kCustom, calls=%fused_computation.2 | custom fusion | bytes 16777280 | tf_op jit(solution)/shard_map/jit(_take)/gather | solution.py:104
  436.3 6.0 %bitcast_select_fusion = f32[4096,512]{1,0:T(8,128)} fusion(f32[16,256,512]{2,1,0:T(8,128)} %gather_fusion.2, pred[4096]{0:T(1024)(128)(4,1)S(1)} %broadcast_in_dim.40), kind=kLoop, calls=%fused_computation.3 | loop fusion | flops 2097152 | bytes 16781312 | tf_op jit(solution)/shard_map/jit(_take)/select_n | solution.py:104
  (16 shorter events, 0.1 us)
Async XLA Ops:
  7.2 11.4 %copy-start = (bf16[256,512]{1,0:T(8,128)(2,1)S(1)}, bf16[256,512]{1,0:T(8,128)(2,1)}, u32[]{:S(2)}) copy-start(bf16[256,512]{1,0:T(8,128)(2,1)} %param.5) | copy-start | bytes 786436
  7.2 169.2 %reduce-scatter.2.cloned.1.call-start = ((), (), s32[]{:S(2)}) async-start(), calls=%async_computation.1 | async-start | bytes 8912896 | tf_op jit(solution)/shard_map/reduce_scatter | solution.py:64
  34.2 394.5 %all-gather.3.cloned.1.call-start = ((), (), s32[]{:S(2)}) async-start(), calls=%async_computation.2 | async-start | bytes 8912896 | tf_op jit(solution)/shard_map/all_gather | solution.py:98
  176.3 12.9 %collective-permute-start = (f32[256,512]{0,1:T(8,128)}, f32[256,512]{0,1:T(8,128)S(1)}, u32[]{:S(2)}, u32[]{:S(2)}) collective-permute-start(f32[256,512]{0,1:T(8,128)} %reduce-scatter.2.cloned.1.call-done), channel_id=1, source_target_pairs={{0,128},{16,144},{32,160},{48,176},{64,192},{80,208},{96,224},{112... | collective-permute-start | bytes 1572872 | tf_op jit(solution)/shard_map/ppermute | solution.py:19
  189.3 1.6 copy-start.3
  196.8 45.2 %copy-start.1 = (f32[512,512]{1,0:T(8,128)}, f32[512,512]{1,0:T(8,128)S(1)}, u32[]{:S(2)}) copy-start(f32[512,512]{1,0:T(8,128)S(1)} %get-tuple-element.13) | copy-start | bytes 3145732
  244.0 1.9 copy-start.2
  252.8 22.3 %collective-permute-start.1 = (f32[512,512]{1,0:T(8,128)S(1)}, f32[512,512]{1,0:T(8,128)S(1)}, u32[]{:S(2)}, u32[]{:S(2)}) collective-permute-start(f32[512,512]{1,0:T(8,128)S(1)} %fusion.47), channel_id=1, source_target_pairs={{0,128},{16,144},{32,160},{48,176},{64,192},{80,208},{96,224},{112... | collective-permute-start | bytes 3145736 | tf_op jit(solution)/shard_map/ppermute | solution.py:19
Sparse Core Ops, SparseCore 0:
  34.3 142.0 reduce-scatter.1
  321.3 107.2 all-gather.2
where the time goes:
time: 450 us; the launch traced here: 449 us
  waiting for transfers between devices  282 us (63%)
  blocking collectives  82.5 us (18%)
  local copies, waits for them, and re-layouts  27.6 us (6%)
  matrix products  27.4 us (6%)
  between operations  16.8 us (4%)
  other arithmetic  10.9 us (2%)
    reduce_scatter x1, waiting for transfers between devices, per_device(): lax.psum_scatter(slot_terms(activations, out_grads, blocks_of, pair_count...  142 us
    all_gather x1, waiting for transfers between devices, per_device(): gathered = lax.all_gather(scaled[None], REP, axis=0, tiled=True)  107 us
    psum x10, blocking collectives, by_axis(): shard = lax.psum(shard, axis)  82.5 us
    ppermute x2, waiting for transfers between devices, partner(): lax.ppermute(shard, axis, [(i, i ^ 1 << stride) for i in range(lax.axis_s...  32.6 us
  transfers between devices with their start and end apart: 4, of which 4 were waited for; matrix products, arithmetic and copies ran while one was open for 0% of the time, Pallas kernels for 0%

commit v1 on v0

--- a/solution.py
+++ b/solution.py
@@ -21,7 +21,7 @@
 
 def by_axis(shard, axes):
     for axis in axes:
-        shard = lax.psum(shard, axis)
+        shard = jnp.sum(lax.all_gather(shard, axis), axis=0)
     return shard
 
 

time: 450 us -> 475 us (1.056)
  local copies, waits for them, and re-layouts: 27.6 us -> 51.4 us
  other arithmetic: 10.9 us -> 20 us
  blocking collectives: 82.5 us -> 76 us
    psum x10 -> x0, blocking collectives: 82.5 us -> none  [by_axis(): shard = lax.psum(shard, axis)]
    unnamed x0 -> x10, blocking collectives: none -> 76 us
    unnamed x9 -> x54, local copies, waits for them, and re-layouts: 4.1 us -> 27.9 us
    reduce_sum x0 -> x15, other arithmetic: none -> 9.17 us  [by_axis(): shard = jnp.sum(lax.all_gather(shard, axis), axis=0)]
  transfers between devices with their start and end apart: 4 -> 4, of which waited for: 4 -> 4; matrix products, arithmetic and copies ran while one was open for 0% -> 1% of each run, Pallas kernels for 0% -> 0%
where the time goes in v1:
time: 475 us; the launch traced here: 474 us
  waiting for transfers between devices  280 us (59%)
  blocking collectives  76 us (16%)
  local copies, waits for them, and re-layouts  51.4 us (11%)
  matrix products  27.3 us (6%)
  other arithmetic  20 us (4%)
  between operations  17 us (4%)
    reduce_scatter x1, waiting for transfers between devices, per_device(): lax.psum_scatter(slot_terms(activations, out_grads, blocks_of, pair_count...  142 us
    all_gather x1, waiting for transfers between devices, per_device(): gathered = lax.all_gather(scaled[None], REP, axis=0, tiled=True)  107 us
    unnamed x10, blocking collectives  76 us
    ppermute x2, waiting for transfers between devices, partner(): lax.ppermute(shard, axis, [(i, i ^ 1 << stride) for i in range(lax.axis_s...  30.5 us
    unnamed x54, local copies, waits for them, and re-layouts  27.9 us
  transfers between devices with their start and end apart: 4, of which 4 were waited for; matrix products, arithmetic and copies ran while one was open for 1% of the time, Pallas kernels for 0%

profile of v1, /device:TPU:1, one launch (start us, length us, event | category | flops | bytes accessed | tf_op | source)
XLA Modules:
  0.0 473.6 jit_solution(12012377691681909627)
XLA Ops:
  8.2 1.3 gather_fusion
  9.6 4.1 copy.26
  13.7 2.8 copy.27
  16.5 2.0 gather_fusion.1
  18.5 6.7 %fusion = f32[16,256,512]{2,1,0:T(8,128)} fusion(bf16[16,256,256]{2,1,0:T(8,128)(2,1)} %gather_fusion.1, pred[16]{0:T(512)(128)(4,1)S(1)} %get-tuple-element.16, bf16[256,512]{1,0:T(8,128)(2,1)S(1)} %copy-done), kind=kOutput, calls=%fused_computation.4 | convolution fusion | flops 1074790400 | bytes 10747920 | tf_op jit(solution)/shard_map/tkp,tc->kpc/dot_general | solution.py:52
  25.2 8.9 %copy.29 = f32[4096,512]{0,1:T(8,128)} copy(f32[4096,512]{1,0:T(8,128)} %bitcast.60) | data formatting | bytes 16777216 | tf_op jit(solution)/shard_map/reshape | solution.py:53
  34.2 142.1 %reduce-scatter.2.cloned.1.call-done = f32[256,512]{0,1:T(8,128)} async-done(((f32[4096,512]{0,1:T(8,128)}), f32[256,512]{0,1:T(8,128)}) %reduce-scatter.2.cloned.1.call-update) | async-done | bytes 524304 | tf_op jit(solution)/shard_map/reduce_scatter | solution.py:64
  176.3 1.2 collective-permute-start
  178.2 11.1 %collective-permute-done = f32[256,512]{0,1:T(8,128)S(1)} collective-permute-done((f32[256,512]{0,1:T(8,128)}, f32[256,512]{0,1:T(8,128)S(1)}, u32[]{:S(2)}, u32[]{:S(2)}) %collective-permute-start) | collective-permute-done | bytes 524320 | tf_op jit(solution)/shard_map/ppermute | solution.py:19
  189.3 1.6 maximum_select_fusion
  191.3 5.5 %select_reduce_fusion = (f32[]{:T(128)}, f32[512,512]{1,0:T(8,128)S(1)}) fusion(f32[512,512]{1,0:T(8,128)S(1)} %copy.31, pred[]{:T(512)S(6)} %lt.75, f32[256,512]{0,1:T(8,128)} %reduce-scatter.2.cloned.1.call-done, f32[256,512]{0,1:T(8,128)} %copy-done.3, f32[1,1,512,512]{3,2,1,0:T(8,128)} %param.6), kind=kOutput, calls=%fused_computation.22 | convolution fusion | flops 1612972032 | bytes 4194309 | tf_op jit(solution)/shard_map/dot_general | solution.py:79
  196.7 1.4 dynamic-update-slice
  198.7 6.0 %all-reduce = f32[4]{0:T(128)S(1)} all-reduce(f32[4]{0:T(128)S(1)} %dynamic-update-slice), channel_id=1, replica_groups=mesh['rep_0'=4,'rep_1'=2,'rep_2'=2,'stripe_0'=4,'stripe_1'=4] {'rep_0'}, use_global_device_ids=true, to_apply=%add | all-reduce | flops 4 | bytes 32
  205.3 1.3 dynamic-update-slice.1
  207.2 7.7 %all-reduce.1 = f32[2]{0:T(128)S(1)} all-reduce(f32[2]{0:T(128)S(1)} %dynamic-update-slice.1), channel_id=1, replica_groups=mesh['rep_0'=4,'rep_1'=2,'rep_2'=2,'stripe_0'=4,'stripe_1'=4] {'rep_1'}, use_global_device_ids=true, to_apply=%add.1 | all-reduce | flops 2 | bytes 16
  215.5 1.4 dynamic-update-slice.2
  217.5 9.1 %all-reduce.2 = f32[2]{0:T(128)S(1)} all-reduce(f32[2]{0:T(128)S(1)} %dynamic-update-slice.2), channel_id=1, replica_groups=mesh['rep_0'=4,'rep_1'=2,'rep_2'=2,'stripe_0'=4,'stripe_1'=4] {'rep_2'}, use_global_device_ids=true, to_apply=%add.2 | all-reduce | flops 2 | bytes 16
  227.3 1.3 dynamic-update-slice.3
  229.3 6.9 %all-reduce.3 = f32[4]{0:T(128)S(1)} all-reduce(f32[4]{0:T(128)S(1)} %dynamic-update-slice.3), channel_id=1, replica_groups=mesh['rep_0'=4,'rep_1'=2,'rep_2'=2,'stripe_0'=4,'stripe_1'=4] {'stripe_0'}, use_global_device_ids=true, to_apply=%add.3 | all-reduce | flops 4 | bytes 32
  236.8 1.3 dynamic-update-slice.4
  238.1 10.1 %all-reduce.4 = f32[4]{0:T(128)S(1)} all-reduce(f32[4]{0:T(128)S(1)} %dynamic-update-slice.4), channel_id=1, replica_groups=mesh['rep_0'=4,'rep_1'=2,'rep_2'=2,'stripe_0'=4,'stripe_1'=4] {'stripe_1'}, use_global_device_ids=true, to_apply=%add.4 | all-reduce | flops 4 | bytes 32
  249.5 0.9 multiply_reduce_fusion
  251.0 2.0 fusion.12
  253.0 1.8 fusion.46
  254.9 1.9 fusion.4
  256.9 3.1 fusion.9
  260.0 1.8 fusion.47
  263.3 1.4 dynamic-update-slice.5
  264.7 19.4 %collective-permute-done.1 = f32[512,512]{1,0:T(8,128)S(1)} collective-permute-done((f32[512,512]{1,0:T(8,128)S(1)}, f32[512,512]{1,0:T(8,128)S(1)}, u32[]{:S(2)}, u32[]{:S(2)}) %collective-permute-start.1) | collective-permute-done | bytes 1048608 | tf_op jit(solution)/shard_map/ppermute | solution.py:19
  284.1 2.7 fusion.15
  286.8 1.8 multiply_reduce_fusion.1
  288.6 1.4 dynamic-update-slice.10
  290.0 6.0 %all-reduce.17 = (f32[4]{0:T(128)S(1)}, f32[4]{0:T(128)S(1)}) all-reduce(f32[4]{0:T(128)S(1)} %dynamic-update-slice.5, f32[4]{0:T(128)S(1)} %dynamic-update-slice.10), channel_id=1, replica_groups=mesh['rep_0'=4,'rep_1'=2,'rep_2'=2,'stripe_0'=4,'stripe_1'=4] {'rep_0'}, use_global_device_ids=true, to_apply=%add.5 | all-reduce | flops 8 | bytes 64
  296.6 1.5 dynamic-update-slice.11
  298.8 1.3 dynamic-update-slice.6
  300.1 7.7 %all-reduce.19 = (f32[2]{0:T(128)S(1)}, f32[2]{0:T(128)S(1)}) all-reduce(f32[2]{0:T(128)S(1)} %dynamic-update-slice.6, f32[2]{0:T(128)S(1)} %dynamic-update-slice.11), channel_id=1, replica_groups=mesh['rep_0'=4,'rep_1'=2,'rep_2'=2,'stripe_0'=4,'stripe_1'=4] {'rep_1'}, use_global_device_ids=true, to_apply=%add.6 | all-reduce | flops 4 | bytes 32
  308.3 1.4 dynamic-update-slice.12
  310.3 1.4 dynamic-update-slice.7
  311.7 9.9 %all-reduce.18 = (f32[2]{0:T(128)S(1)}, f32[2]{0:T(128)S(1)}) all-reduce(f32[2]{0:T(128)S(1)} %dynamic-update-slice.7, f32[2]{0:T(128)S(1)} %dynamic-update-slice.12), channel_id=1, replica_groups=mesh['rep_0'=4,'rep_1'=2,'rep_2'=2,'stripe_0'=4,'stripe_1'=4] {'rep_2'}, use_global_device_ids=true, to_apply=%add.7 | all-reduce | flops 4 | bytes 32
  322.2 1.4 dynamic-update-slice.13
  324.2 1.4 dynamic-update-slice.8
  325.6 6.1 %all-reduce.16 = (f32[4]{0:T(128)S(1)}, f32[4]{0:T(128)S(1)}) all-reduce(f32[4]{0:T(128)S(1)} %dynamic-update-slice.8, f32[4]{0:T(128)S(1)} %dynamic-update-slice.13), channel_id=1, replica_groups=mesh['rep_0'=4,'rep_1'=2,'rep_2'=2,'stripe_0'=4,'stripe_1'=4] {'stripe_0'}, use_global_device_ids=true, to_apply=%add.8 | all-reduce | flops 8 | bytes 64
  332.3 1.4 dynamic-update-slice.14
  334.3 1.4 dynamic-update-slice.9
  335.6 6.6 %all-reduce.15 = (f32[4]{0:T(128)S(1)}, f32[4]{0:T(128)S(1)}) all-reduce(f32[4]{0:T(128)S(1)} %dynamic-update-slice.9, f32[4]{0:T(128)S(1)} %dynamic-update-slice.14), channel_id=1, replica_groups=mesh['rep_0'=4,'rep_1'=2,'rep_2'=2,'stripe_0'=4,'stripe_1'=4] {'stripe_1'}, use_global_device_ids=true, to_apply=%add.9 | all-reduce | flops 8 | bytes 64
  345.8 107.2 %all-gather.3.cloned.1.call-done = f32[4096,512]{1,0:T(8,128)} async-done(((f32[256,512]{1,0:T(8,128)}), f32[4096,512]{1,0:T(8,128)}) %all-gather.3.cloned.1.call-update) | async-done | bytes 8388624 | tf_op jit(solution)/shard_map/all_gather | solution.py:98
  453.1 7.7 %gather_fusion.2 = f32[16,256,512]{2,1,0:T(8,128)} fusion(f32[16,256,512]{2,1,0:T(8,128)} %bitcast.61, s32[1024]{0:T(1024)S(1)} %pad_clamp_fusion), kind=kCustom, calls=%fused_computation.2 | custom fusion | bytes 16777280 | tf_op jit(solution)/shard_map/jit(_take)/gather | solution.py:104
  460.7 6.0 %bitcast_select_fusion = f32[4096,512]{1,0:T(8,128)} fusion(f32[16,256,512]{2,1,0:T(8,128)} %gather_fusion.2, pred[4096]{0:T(1024)(128)(4,1)S(1)} %broadcast_in_dim.40), kind=kLoop, calls=%fused_computation.3 | loop fusion | flops 2097152 | bytes 16781312 | tf_op jit(solution)/shard_map/jit(_take)/select_n | solution.py:104
  (76 shorter events, 16.2 us)
Async XLA Ops:
  7.2 11.4 %copy-start = (bf16[256,512]{1,0:T(8,128)(2,1)S(1)}, bf16[256,512]{1,0:T(8,128)(2,1)}, u32[]{:S(2)}) copy-start(bf16[256,512]{1,0:T(8,128)(2,1)} %param.5) | copy-start | bytes 786436
  7.2 169.2 %reduce-scatter.2.cloned.1.call-start = ((), (), s32[]{:S(2)}) async-start(), calls=%async_computation.1 | async-start | bytes 8912896 | tf_op jit(solution)/shard_map/reduce_scatter | solution.py:64
  34.1 143.4 %copy-start.8 = (u32[256]{0:T(256)S(1)}, u32[256]{0:T(256)}, u32[]{:S(2)}) copy-start(u32[256]{0:T(256)} %constant.146) | copy-start | bytes 3076
  34.2 418.9 %all-gather.3.cloned.1.call-start = ((), (), s32[]{:S(2)}) async-start(), calls=%async_computation.2 | async-start | bytes 8912896 | tf_op jit(solution)/shard_map/all_gather | solution.py:98
  176.3 12.9 %collective-permute-start = (f32[256,512]{0,1:T(8,128)}, f32[256,512]{0,1:T(8,128)S(1)}, u32[]{:S(2)}, u32[]{:S(2)}) collective-permute-start(f32[256,512]{0,1:T(8,128)} %reduce-scatter.2.cloned.1.call-done), channel_id=1, source_target_pairs={{0,128},{16,144},{32,160},{48,176},{64,192},{80,208},{96,224},{112... | collective-permute-start | bytes 1572872 | tf_op jit(solution)/shard_map/ppermute | solution.py:19
  189.3 1.6 copy-start.3
  191.2 6.9 %copy-start.7 = (u32[256]{0:T(256)S(1)}, u32[256]{0:T(256)}, u32[]{:S(2)}) copy-start(u32[256]{0:T(256)} %constant.151) | copy-start | bytes 3076
  191.2 15.4 %copy-start.6 = (u32[256]{0:T(256)S(1)}, u32[256]{0:T(256)}, u32[]{:S(2)}) copy-start(u32[256]{0:T(256)} %constant.156) | copy-start | bytes 3076
  191.2 25.7 %copy-start.5 = (u32[256]{0:T(256)S(1)}, u32[256]{0:T(256)}, u32[]{:S(2)}) copy-start(u32[256]{0:T(256)} %constant.161) | copy-start | bytes 3076
  191.2 37.4 %copy-start.4 = (u32[256]{0:T(256)S(1)}, u32[256]{0:T(256)}, u32[]{:S(2)}) copy-start(u32[256]{0:T(256)} %constant.166) | copy-start | bytes 3076
  196.7 54.3 %copy-start.1 = (f32[512,512]{1,0:T(8,128)}, f32[512,512]{1,0:T(8,128)S(1)}, u32[]{:S(2)}) copy-start(f32[512,512]{1,0:T(8,128)S(1)} %get-tuple-element.13) | copy-start | bytes 3145732
  253.0 1.9 copy-start.2
  261.9 22.3 %collective-permute-start.1 = (f32[512,512]{1,0:T(8,128)S(1)}, f32[512,512]{1,0:T(8,128)S(1)}, u32[]{:S(2)}, u32[]{:S(2)}) collective-permute-start(f32[512,512]{1,0:T(8,128)S(1)} %fusion.47), channel_id=1, source_target_pairs={{0,128},{16,144},{32,160},{48,176},{64,192},{80,208},{96,224},{112... | collective-permute-start | bytes 3145736 | tf_op jit(solution)/shard_map/ppermute | solution.py:19
Sparse Core Ops, SparseCore 0:
  34.3 142.0 reduce-scatter.1
  345.7 107.2 all-gather.2
